TPU v7x, 256 devices: a whole 4x4x8 slice. The times are simulated.
256 devices in a mesh: gx: 4 (over z_lo), gy: 4 (over y), gz: 16 (over x, z_hi, core).
Axes of the slice: x: 4, y: 4, z: 8 (z_hi: 2, z_lo: 4; z = z_hi * 4 + z_lo), core: 2. Of those that a mesh axis runs over, the one named last changes fastest.
Arguments:
- factor_inv: bfloat16 [4, 4096, 16384], P('gx', 'gy', 'gz')
- sep_sizes: int32 [4, 4, 16], P('gx', 'gy', 'gz'), may hold values from 512 to 1024
- coupling: bfloat16 [12, 4096, 16384], P('gx', 'gy', 'gz'), may hold values from -0.109375 to 0.109375
Outputs:
- schur_update: float32 [4, 4096, 16384], P('gx', 'gy', 'gz')
All inputs are finite; a program needn't handle non-finite values.
Results may differ from a plain program's by a relative error of at most 0.0023.
Values may be sent and summed in bfloat16 or wider, within the bound.
A program may use at most 128 MiB of HBM per device.

v0:
```python
import jax
import jax.numpy as jnp
from jax import lax
from jax.sharding import PartitionSpec as P


def passed_along(block, axis, distance):
    devices = range(lax.axis_size(axis))
    route = [(i - distance, i) for i in devices if i - distance in devices]
    return lax.ppermute(block, axis, route)


def square_of(solved):
    return lax.dot_general(
        solved, solved, (((0,), (0,)), ((), ())), preferred_element_type=jnp.float32
    )


def update_of(factor, couple):
    solved = jnp.dot(factor, couple, preferred_element_type=jnp.float32).astype(jnp.bfloat16)
    return square_of(solved)


def on_device(factor_inv, sep_sizes, coupling):
    width = factor_inv.shape[1]
    inner = jnp.arange(width, dtype=jnp.int32)
    keep = (inner < sep_sizes[0, 0, 0]).astype(jnp.bfloat16)
    masked = factor_inv[0] * keep[:, None] * keep[None, :]
    below_z = passed_along(masked, "gz", 1)
    above_z = passed_along(masked, "gz", -1)
    below_y = passed_along(masked, "gy", 1)
    total = update_of(below_z, coupling[0])
    total = total + update_of(above_z, coupling[1])
    total = total + update_of(below_y, coupling[2])
    return total[None]


def solution(mesh):
    return jax.shard_map(
        on_device,
        mesh=mesh,
        in_specs=(P("gx", "gy", "gz"), P("gx", "gy", "gz"), P("gx", "gy", "gz")),
        out_specs=P("gx", "gy", "gz"),
        check_vma=False,
    )
```

profile of v0, /device:TPU:197, one launch (start us, length us, event | category | flops | bytes accessed | tf_op | source)
XLA Modules:
  0.0 132.7 jit_solution(6516174092609081375)
XLA Ops:
  0.7 1.8 %fusion.6 = bf16[1024,1024]{1,0:T(8,128)(2,1)S(1)} fusion(bf16[1,1024,1024]{2,1,0:T(8,128)(2,1)} %param.3, bf16[1024]{0:T(1024)(128)(2,1)S(1)} %fusion.30), kind=kLoop, calls=%fused_computation.8 | loop fusion | flops 2097152 | bytes 4196352 | tf_op jit(solution)/shard_map/mul | solution.py:28
  2.5 4.5 %collective-permute-start.2 = (bf16[1024,1024]{1,0:T(8,128)(2,1)S(1)}, bf16[1024,1024]{1,0:T(8,128)(2,1)}, u32[]{:S(2)}, u32[]{:S(2)}) collective-permute-start(bf16[1024,1024]{1,0:T(8,128)(2,1)S(1)} %fusion.6), channel_id=1, source_target_pairs={{0,16},{16,32},{32,48},{1,17},{17,33},{33,49},{2,18},{18,34},{34,5... | collective-permute-start | bytes 6291464 | tf_op jit(solution)/shard_map/ppermute | solution.py:10
  7.1 2.9 %collective-permute-start.1 = (bf16[1024,1024]{1,0:T(8,128)(2,1)S(1)}, bf16[1024,1024]{1,0:T(8,128)(2,1)}, u32[]{:S(2)}, u32[]{:S(2)}) collective-permute-start(bf16[1024,1024]{1,0:T(8,128)(2,1)S(1)} %fusion.6), channel_id=1, source_target_pairs={{1,0},{2,1},{3,2},{4,3},{5,4},{6,5},{7,6},{8,7},{9,8},{10,9},{11,1... | collective-permute-start | bytes 6291464 | tf_op jit(solution)/shard_map/ppermute | solution.py:10
  9.9 7.5 %collective-permute-start = (bf16[1024,1024]{1,0:T(8,128)(2,1)S(1)}, bf16[1024,1024]{1,0:T(8,128)(2,1)}, u32[]{:S(2)}, u32[]{:S(2)}) collective-permute-start(bf16[1024,1024]{1,0:T(8,128)(2,1)S(1)} %fusion.6), channel_id=1, source_target_pairs={{0,1},{1,2},{2,3},{3,4},{4,5},{5,6},{6,7},{7,8},{8,9},{9,10},{10,1... | collective-permute-start | bytes 6291464 | tf_op jit(solution)/shard_map/ppermute | solution.py:10
  17.4 32.6 %collective-permute-done.2 = bf16[1024,1024]{1,0:T(8,128)(2,1)} collective-permute-done((bf16[1024,1024]{1,0:T(8,128)(2,1)S(1)}, bf16[1024,1024]{1,0:T(8,128)(2,1)}, u32[]{:S(2)}, u32[]{:S(2)}) %collective-permute-start.2) | collective-permute-done | bytes 2097184 | tf_op jit(solution)/shard_map/ppermute | solution.py:10
  50.0 12.2 %fusion.7 = f32[1024,1024]{1,0:T(8,128)} fusion(bf16[1024,1024]{1,0:T(8,128)(2,1)} %collective-permute-done.2, bf16[3,1024,1024]{2,1,0:T(8,128)(2,1)} %param.5), kind=kOutput, calls=%fused_computation.9 | convolution fusion | flops 4296015872 | bytes 8388608 | tf_op jit(solution)/shard_map/dot_general | solution.py:14
  62.2 43.5 %collective-permute-done.1 = bf16[1024,1024]{1,0:T(8,128)(2,1)} collective-permute-done((bf16[1024,1024]{1,0:T(8,128)(2,1)S(1)}, bf16[1024,1024]{1,0:T(8,128)(2,1)}, u32[]{:S(2)}, u32[]{:S(2)}) %collective-permute-start.1) | collective-permute-done | bytes 2097184 | tf_op jit(solution)/shard_map/ppermute | solution.py:10
  105.7 12.2 %fusion.10 = f32[1024,1024]{1,0:T(8,128)} fusion(bf16[1024,1024]{1,0:T(8,128)(2,1)} %collective-permute-done.1, bf16[3,1024,1024]{2,1,0:T(8,128)(2,1)} %param.5), kind=kOutput, calls=%fused_computation.12 | convolution fusion | flops 4296015872 | bytes 8388608 | tf_op jit(solution)/shard_map/dot_general | solution.py:14
  117.9 0.0 collective-permute-done
  117.9 14.8 %add_bitcast_fusion = f32[1,1024,1024]{2,1,0:T(8,128)} fusion(f32[1024,1024]{1,0:T(8,128)} %fusion.7, f32[1024,1024]{1,0:T(8,128)} %fusion.10, bf16[1024,1024]{1,0:T(8,128)(2,1)} %collective-permute-done, bf16[3,1024,1024]{2,1,0:T(8,128)(2,1)} %param.5), kind=kOutput, calls=%fused_computation | convolution fusion | flops 4298113024 | bytes 16777216 | tf_op jit(solution)/shard_map/dot_general | solution.py:14
  (1 shorter events, 0.0 us)
Async XLA Ops:
  2.5 47.5 %collective-permute-start.2 = (bf16[1024,1024]{1,0:T(8,128)(2,1)S(1)}, bf16[1024,1024]{1,0:T(8,128)(2,1)}, u32[]{:S(2)}, u32[]{:S(2)}) collective-permute-start(bf16[1024,1024]{1,0:T(8,128)(2,1)S(1)} %fusion.6), channel_id=1, source_target_pairs={{0,16},{16,32},{32,48},{1,17},{17,33},{33,49},{2,18},{18,34},{34,5... | collective-permute-start | bytes 6291464 | tf_op jit(solution)/shard_map/ppermute | solution.py:10
  7.1 98.7 %collective-permute-start.1 = (bf16[1024,1024]{1,0:T(8,128)(2,1)S(1)}, bf16[1024,1024]{1,0:T(8,128)(2,1)}, u32[]{:S(2)}, u32[]{:S(2)}) collective-permute-start(bf16[1024,1024]{1,0:T(8,128)(2,1)S(1)} %fusion.6), channel_id=1, source_target_pairs={{1,0},{2,1},{3,2},{4,3},{5,4},{6,5},{7,6},{8,7},{9,8},{10,9},{11,1... | collective-permute-start | bytes 6291464 | tf_op jit(solution)/shard_map/ppermute | solution.py:10
  9.9 108.0 %collective-permute-start = (bf16[1024,1024]{1,0:T(8,128)(2,1)S(1)}, bf16[1024,1024]{1,0:T(8,128)(2,1)}, u32[]{:S(2)}, u32[]{:S(2)}) collective-permute-start(bf16[1024,1024]{1,0:T(8,128)(2,1)S(1)} %fusion.6), channel_id=1, source_target_pairs={{0,1},{1,2},{2,3},{3,4},{4,5},{5,6},{6,7},{7,8},{8,9},{9,10},{10,1... | collective-permute-start | bytes 6291464 | tf_op jit(solution)/shard_map/ppermute | solution.py:10
where the time goes:
time: 133 us
  waiting for transfers between devices  76.1 us (57%)
  matrix products  39.1 us (29%)
  starting transfers between devices  14.9 us (11%)
  other arithmetic  1.85 us (1%)
    ppermute x3, waiting for transfers between devices, passed_along(): return lax.ppermute(block, axis, route)  76.1 us
    dot_general x3, matrix products, square_of(): lax.dot_general(solved, solved, (((0,), (0,)), ((), ())), preferred_eleme...  39.1 us
    ppermute x3, starting transfers between devices, passed_along(): return lax.ppermute(block, axis, route)  14.9 us
  transfers between devices with their start and end apart: 3, of which 2 were waited for; matrix products, arithmetic and copies ran while one was open for 18% of the time, Pallas kernels for 0%

commit v1 on v0

v1 whole, which is shorter than its diff:
```python
import jax
import jax.numpy as jnp
from jax import lax
from jax.experimental import pallas as pl
from jax.experimental.pallas import tpu as pltpu
from jax.sharding import PartitionSpec as P

MESH = pl.DeviceIdType.MESH
BF = jnp.bfloat16
F32 = jnp.float32
B = 256
CROSS, PARTNER, BELOW = 0, 1, 2
SMALL = 4
TN = (((0,), (0,)), ((), ()))


def tri(shape):
    return lax.broadcasted_iota(jnp.int32, shape, 0), lax.broadcasted_iota(jnp.int32, shape, 1)


def gram_rows(g, u):
    return lax.dot_general(g[:, u * B:(u + 1) * B], g[:, u * B:], TN, preferred_element_type=F32)


def packed(lower, upper):
    row, col = tri((B, B))
    return jnp.where(row > col, lower, jnp.where(row == col, 0.5 * upper, upper))


def half_diagonal(block):
    row, col = tri((B, B))
    return jnp.sum(jnp.where(row == col, 0.5 * block, 0.0), axis=0, keepdims=True)


def exchange(f_hbm, n_ref, c_hbm, t_ref, g, c, z, half, left, right, sbuf, ssmall, rbuf, rsmall, pbuf,
             sems, send_sem, recv_sem, small_send, small_recv, pass_send, pass_recv):
    zlo, y, gz = lax.axis_index("gx"), lax.axis_index("gy"), lax.axis_index("gz")
    size_y, size_z = lax.axis_size("gy"), lax.axis_size("gz")
    core, x, kind = lax.rem(gz, 2), gz // 4, lax.rem(gz, 4)
    partner = gz + 1 - 2 * core
    cross = gz - 1 + 2 * core
    has_cross = (cross >= 0) & (cross < size_z)
    has_up, has_below = y < size_y - 1, y > 0

    steps = size_z // 4
    outer = (kind == 3) | (kind == 0)
    forward = kind == 3
    has_right, has_left = outer & (x < steps - 1), outer & (x > 0)
    n_passed = jnp.where(has_cross & outer, jnp.where(forward, x + 1, steps - x), 0)
    n_passing = jnp.where(outer, jnp.where(forward, x, steps - 1 - x), 0)
    passer = gz + jnp.where(forward, 4, -4)
    receiver = gz + jnp.where(forward, -3, 3)

    def at(col, row=None):
        row = y if row is None else jnp.clip(row, 0, size_y - 1)
        return (zlo, row, jnp.clip(col, 0, size_z - 1))

    sends_to = {CROSS: at(cross), PARTNER: at(partner), BELOW: at(gz, y + 1)}
    sends = {CROSS: has_cross, PARTNER: gz >= 0, BELOW: has_up}
    gets = {CROSS: has_cross, PARTNER: gz >= 0, BELOW: has_below}
    slot_of = {CROSS: core, PARTNER: 1 - core, BELOW: 2}

    load_f = pltpu.make_async_copy(f_hbm.at[0], g, sems.at[0])
    load_f.start()

    barrier = pltpu.get_barrier_semaphore()
    peers = [(has_cross, at(cross)), (outer, at(receiver)), (has_right, at(gz + 4)), (has_left, at(gz - 4)),
             (has_up, at(gz, y + 1)), (has_below, at(gz, y - 1)), (gz >= 0, at(partner))]
    for present, device in peers:
        @pl.when(present)
        def _():
            pl.semaphore_signal(barrier, inc=1, device_id=device, device_id_type=MESH)
    n_peers = sum(present.astype(jnp.int32) for present, _ in peers)

    load_c = [pltpu.make_async_copy(c_hbm.at[e], c.at[e], sems.at[1 + e]) for e in range(3)]
    for copy in load_c:
        copy.start()

    def message(to, m):
        if m == SMALL:
            return pltpu.make_async_remote_copy(
                src_ref=ssmall, dst_ref=rsmall.at[to], send_sem=small_send.at[to], recv_sem=small_recv.at[to],
                device_id=sends_to[to], device_id_type=MESH)
        return pltpu.make_async_remote_copy(
            src_ref=sbuf.at[m], dst_ref=rbuf.at[to, m], send_sem=send_sem.at[to, m], recv_sem=recv_sem.at[to, m],
            device_id=sends_to[to], device_id_type=MESH)

    def to_passer(m):
        return pltpu.make_async_remote_copy(
            src_ref=sbuf.at[m], dst_ref=pbuf.at[m - 1], send_sem=send_sem.at[CROSS, m], recv_sem=pass_recv.at[m - 1],
            device_id=at(passer), device_id_type=MESH)

    def passed_on(m):
        return pltpu.make_async_remote_copy(
            src_ref=pbuf.at[m - 1], dst_ref=rbuf.at[CROSS, m], send_sem=pass_send.at[m - 1], recv_sem=recv_sem.at[CROSS, m],
            device_id=at(receiver), device_id_type=MESH)

    def send(m):
        if m in (0, SMALL):
            @pl.when(has_cross)
            def _():
                message(CROSS, m).start()
        else:
            @pl.when(has_cross & (m < 4 - n_passed))
            def _():
                message(CROSS, m).start()

            @pl.when(m >= 4 - n_passed)
            def _():
                to_passer(m).start()
        for to in (BELOW, PARTNER):
            @pl.when(sends[to])
            def _():
                message(to, m).start()

    def pass_on(m):
        @pl.when(m >= 4 - n_passing)
        def _():
            to_passer(m).wait_recv()
            passed_on(m).start()

    load_f.wait()
    n = n_ref[0, 0, 0]
    rows, width = 128, g.shape[1]

    def mask(i, most):
        at_rows = pl.ds(pl.multiple_of(i * rows, rows), rows)
        row, col = tri((rows, width))
        kept = jnp.where((row + i * rows < n) & (col < n), g[at_rows, :].astype(F32), 0.0)
        g[at_rows, :] = kept.astype(BF)
        return jnp.maximum(most, jnp.max(jnp.abs(kept), axis=0, keepdims=True))

    most = lax.fori_loop(0, g.shape[0] // rows, mask, jnp.zeros((1, width), F32))
    power = jnp.clip(jnp.floor(jnp.log2(jnp.maximum(most, 1e-36))), -120.0, 120.0)
    scale, inverse = jnp.exp2(power).astype(BF).astype(F32), jnp.exp2(-power).astype(BF).astype(F32)

    @pl.loop(0, g.shape[0] // rows)
    def _(i):
        at_rows = pl.ds(pl.multiple_of(i * rows, rows), rows)
        g[at_rows, :] = (g[at_rows, :].astype(F32) * inverse).astype(BF)

    h0 = gram_rows(g, 0)
    sbuf[0] = h0[:, B:3 * B].astype(BF)
    sbuf[1, :, :B] = h0[:, 3 * B:].astype(BF)
    d0 = half_diagonal(h0[:, :B])
    low0 = h0[:, :B]
    pl.semaphore_wait(barrier, n_peers)
    send(0)
    h1 = gram_rows(g, 1)
    sbuf[1, :, B:] = packed(low0, h1[:, :B]).astype(BF)
    sbuf[3] = h1[:, B:].astype(BF)
    send(1)
    h2 = gram_rows(g, 2)
    sbuf[2, :, :B] = h2[:, B:].astype(BF)
    h3 = gram_rows(g, 3)
    sbuf[2, :, B:] = packed(h2[:, :B], h3).astype(BF)
    d2 = half_diagonal(h2[:, :B])
    lines = [scale[:, 128 * p:128 * (p + 1)] for p in range(8)]
    lines += [d0[:, :128], d0[:, 128:], d2[:, :128], d2[:, 128:]]
    for p, line in enumerate(lines):
        ssmall[p:p + 1, :] = line
    ssmall[12:16, :] = jnp.zeros((4, 128), F32)
    send(SMALL)
    send(2)
    send(3)

    t_ref[...] = jnp.zeros_like(t_ref)
    for copy in load_c:
        copy.wait()

    def scale_c(frm):
        slot = slot_of[frm]
        for p in range(8):
            line = rsmall[frm, p:p + 1, :]
            column = jnp.transpose(jnp.broadcast_to(line, (128, 128)))
            at_rows = pl.ds(128 * p, 128)

            @pl.loop(0, 8)
            def _(q):
                cols = pl.ds(pl.multiple_of(q * 128, 128), 128)
                c[slot, at_rows, cols] = (c[slot, at_rows, cols].astype(F32) * column).astype(BF)

    def half_block(frm, u):
        row, col = tri((B, B))
        both = rbuf[frm, 1 if u < 2 else 2, :, B:].astype(F32)
        if u % 2 == 1:
            half[...] = jnp.where(row <= col, both, 0.0).astype(BF)
        else:
            line = jnp.concatenate([rsmall[frm, 8 + u:9 + u, :], rsmall[frm, 9 + u:10 + u, :]], axis=1)
            half[...] = jnp.where(row > col, both, jnp.where(row == col, jnp.broadcast_to(line, (B, B)), 0.0)).astype(BF)

    def consume(frm, u):
        slot = slot_of[frm]
        half_block(frm, u)
        rest = {
            0: [(rbuf.at[frm, 0], 1, 3), (rbuf.at[frm, 1, :, pl.ds(0, B)], 3, 4)],
            1: [(rbuf.at[frm, 3], 2, 4)],
            2: [(rbuf.at[frm, 2, :, pl.ds(0, B)], 3, 4)],
            3: [],
        }[u]
        for nt in range(2):
            cols = slice(512 * nt, 512 * (nt + 1))
            acc = jnp.dot(half[...], c[slot, u * B:(u + 1) * B, cols], preferred_element_type=F32)
            for factor, lo, hi in rest:
                acc += jnp.dot(factor[...], c[slot, lo * B:hi * B, cols], preferred_element_type=F32)
            z[:, cols] = acc.astype(BF)

        @pl.loop(0, 4)
        def _(i):
            cols = pl.ds(pl.multiple_of(i * B, B), B)
            t_ref[cols, :] += lax.dot_general(c[slot, u * B:(u + 1) * B, cols], z[...], TN, preferred_element_type=F32)

    def wait_for(frm, *messages):
        for m in messages:
            message(frm, m).wait_recv()

    def early(frm):
        wait_for(frm, 0, 1, SMALL)
        scale_c(frm)
        consume(frm, 0)

    def middle(frm):
        wait_for(frm, 2)
        consume(frm, 2)
        consume(frm, 3)

    def late(frm):
        wait_for(frm, 3)
        consume(frm, 1)

    early(PARTNER)
    pass_on(1)
    middle(PARTNER)
    pass_on(2)
    late(PARTNER)
    pass_on(3)

    @pl.when(has_below)
    def _():
        early(BELOW)
        middle(BELOW)

    @pl.when(has_cross)
    def _():
        early(CROSS)

    @pl.when(has_below)
    def _():
        late(BELOW)

    @pl.when(has_cross)
    def _():
        middle(CROSS)
        half_block(CROSS, 1)
        slot = slot_of[CROSS]
        right[B:, :] = c[slot, B:2 * B, :]

        @pl.loop(0, 4)
        def _(i):
            cols = pl.ds(pl.multiple_of(i * B, B), B)
            left[cols, :B] = jnp.transpose(c[slot, B:2 * B, cols])

    for gap in range(4):
        @pl.loop(0, 4 - gap)
        def _(i):
            one = pl.ds(pl.multiple_of(i * B, B), B)
            two = pl.ds(pl.multiple_of((i + gap) * B, B), B)
            upper, lower = t_ref[one, two], t_ref[two, one]
            t_ref[one, two] = upper + jnp.transpose(lower)
            if gap:
                t_ref[two, one] = lower + jnp.transpose(upper)

    @pl.when(has_cross)
    def _():
        slot = slot_of[CROSS]
        wait_for(CROSS, 3)
        for i in range(4):
            cols = slice(i * B, (i + 1) * B)
            acc = jnp.dot(half[...], c[slot, B:2 * B, cols], preferred_element_type=F32)
            acc += jnp.dot(rbuf[CROSS, 3], c[slot, 2 * B:, cols], preferred_element_type=F32)
            right[:B, cols] = acc.astype(BF)
            left[cols, B:] = jnp.transpose(acc).astype(BF)

        @pl.loop(0, 4)
        def _(i):
            cols = pl.ds(pl.multiple_of(i * B, B), B)
            t_ref[cols, :] += jnp.dot(left[cols, :], right[...], preferred_element_type=F32)

    for to in (CROSS, PARTNER, BELOW):
        @pl.when(sends[to])
        def _():
            for m in range(5):
                message(to, m).wait_send()
    for m in (1, 2, 3):
        @pl.when(m >= 4 - n_passing)
        def _():
            passed_on(m).wait_send()


def on_device(factor_inv, sep_sizes, coupling):
    width, m = factor_inv.shape[1], coupling.shape[2]
    update = pl.pallas_call(
        exchange,
        out_shape=pltpu.VMEM((m, m), F32),
        in_specs=[pl.BlockSpec(memory_space=pl.ANY), pl.BlockSpec(memory_space=pltpu.SMEM), pl.BlockSpec(memory_space=pl.ANY)],
        out_specs=pl.BlockSpec(memory_space=pltpu.VMEM),
        scratch_shapes=[
            pltpu.VMEM((width, width), BF),
            pltpu.VMEM((3, width, m), BF),
            pltpu.VMEM((B, m), BF),
            pltpu.VMEM((B, B), BF),
            pltpu.VMEM((m, 2 * B), BF),
            pltpu.VMEM((2 * B, m), BF),
            pltpu.VMEM((4, B, 2 * B), BF),
            pltpu.VMEM((16, 128), F32),
            pltpu.VMEM((3, 4, B, 2 * B), BF),
            pltpu.VMEM((3, 16, 128), F32),
            pltpu.VMEM((3, B, 2 * B), BF),
            pltpu.SemaphoreType.DMA((4,)),
            pltpu.SemaphoreType.DMA((3, 4)),
            pltpu.SemaphoreType.DMA((3, 4)),
            pltpu.SemaphoreType.DMA((3,)),
            pltpu.SemaphoreType.DMA((3,)),
            pltpu.SemaphoreType.DMA((3,)),
            pltpu.SemaphoreType.DMA((3,)),
        ],
        compiler_params=pltpu.CompilerParams(collective_id=0, has_side_effects=True, vmem_limit_bytes=48 * 1024 * 1024),
        name="exchange",
    )(factor_inv, sep_sizes, coupling)
    return update[None]


def solution(mesh):
    spec = P("gx", "gy", "gz")
    return jax.shard_map(on_device, mesh=mesh, in_specs=(spec, spec, spec), out_specs=spec, check_vma=False)
```

time: 133 us -> 57.1 us (0.43)
  the two profiles are of different devices: /device:TPU:197 before, /device:TPU:45 now
where the time goes in v1:
time: 57.1 us; the launch traced here: 56.8 us
  Pallas kernels  54.1 us (95%)
  local copies, waits for them, and re-layouts  2.02 us (4%)
  between operations  0.66 us (1%)
    pallas_call x1, Pallas kernels, on_device(): pl.pallas_call(exchange, out_shape=pltpu.VMEM((m, m), F32), in_specs=[pl....  54.1 us
    unnamed x1, local copies, waits for them, and re-layouts  2.02 us

profile of v1, /device:TPU:45, one launch (start us, length us, event | category | flops | bytes accessed | tf_op | source)
XLA Modules:
  0.0 56.8 jit_solution(12780007924298117011)
XLA Ops:
  0.7 54.1 %exchange.1 = f32[1024,1024]{1,0:T(8,128)S(1)} custom-call(bf16[1,1024,1024]{2,1,0:T(8,128)(2,1)} %f_hbm.1, s32[1,1,1]{2,1,0:T(1,128)S(6)} %copy.6.n_ref, bf16[3,1024,1024]{2,1,0:T(8,128)(2,1)} %c_hbm.1), custom_call_target="tpu_custom_call" | custom-call | tf_op jit(solution)/shard_map/exchange/pallas_call | solution.py:302
  54.8 2.0 %copy.5 = f32[1,1024,1024]{2,1,0:T(8,128)} copy(f32[1,1024,1024]{2,1,0:T(8,128)S(1)} %bitcast.1) | data formatting | bytes 8388608

commit v2 on v1

v2 whole, which is shorter than its diff:
```python
import jax
import jax.numpy as jnp
from jax import lax
from jax.experimental import pallas as pl
from jax.experimental.pallas import tpu as pltpu
from jax.sharding import PartitionSpec as P

MESH = pl.DeviceIdType.MESH
BF = jnp.bfloat16
F32 = jnp.float32
B = 256
CROSS, PARTNER, BELOW = 0, 1, 2
SMALL = 4
TN = (((0,), (0,)), ((), ()))
NT = (((1,), (1,)), ((), ()))


def tri(shape):
    return lax.broadcasted_iota(jnp.int32, shape, 0), lax.broadcasted_iota(jnp.int32, shape, 1)


def gram(g, u, lo, hi):
    return lax.dot_general(g[:, u * B:(u + 1) * B], g[:, lo * B:hi * B], TN, preferred_element_type=F32)


def packed(lower, upper):
    row, col = tri((B, B))
    return jnp.where(row > col, lower, jnp.where(row == col, 0.5 * upper, upper))


def half_diagonal(block):
    row, col = tri((B, B))
    return jnp.sum(jnp.where(row == col, 0.5 * block, 0.0), axis=0, keepdims=True)


def exchange(f_hbm, n_hbm, c_hbm, t_ref, left, right, g, c, z, half, ct, zt, zp, n_ref, sbuf, ssmall, rbuf, rsmall, pbuf,
             f_sem, sems, send_sem, recv_sem, small_send, small_recv, pass_send, pass_recv):
    zlo, y, gz = lax.axis_index("gx"), lax.axis_index("gy"), lax.axis_index("gz")
    size_y, size_z = lax.axis_size("gy"), lax.axis_size("gz")
    core, x, kind = lax.rem(gz, 2), gz // 4, lax.rem(gz, 4)
    partner = gz + 1 - 2 * core
    cross = gz - 1 + 2 * core
    has_cross = (cross >= 0) & (cross < size_z)
    has_up, has_below = y < size_y - 1, y > 0

    steps = size_z // 4
    outer = (kind == 3) | (kind == 0)
    forward = kind == 3
    has_right, has_left = outer & (x < steps - 1), outer & (x > 0)
    n_passed = jnp.where(has_cross & outer, jnp.where(forward, x + 1, steps - x), 0)
    n_passing = jnp.where(outer, jnp.where(forward, x, steps - 1 - x), 0)
    passer = gz + jnp.where(forward, 4, -4)
    receiver = gz + jnp.where(forward, -3, 3)

    def at(col, row=None):
        row = y if row is None else jnp.clip(row, 0, size_y - 1)
        return (zlo, row, jnp.clip(col, 0, size_z - 1))

    sends_to = {CROSS: at(cross), PARTNER: at(partner), BELOW: at(gz, y + 1)}
    sends = {CROSS: has_cross, PARTNER: gz >= 0, BELOW: has_up}
    gets = {CROSS: has_cross, PARTNER: gz >= 0, BELOW: has_below}
    slot_of = {CROSS: core, PARTNER: 1 - core, BELOW: 2}

    rows, width = 128, g.shape[1]
    blocks = g.shape[0] // rows
    load_n = pltpu.make_async_copy(n_hbm, n_ref, sems.at[0])
    load_n.start()
    load_f = [pltpu.make_async_copy(f_hbm.at[0, pl.ds(rows * i, rows)], g.at[pl.ds(rows * i, rows)], f_sem.at[i]) for i in range(blocks)]
    for copy in load_f:
        copy.start()

    barrier = pltpu.get_barrier_semaphore()
    peers = [(has_cross, at(cross)), (outer, at(receiver)), (has_right, at(gz + 4)), (has_left, at(gz - 4)),
             (has_up, at(gz, y + 1)), (has_below, at(gz, y - 1)), (gz >= 0, at(partner))]
    for present, device in peers:
        @pl.when(present)
        def _():
            pl.semaphore_signal(barrier, inc=1, device_id=device, device_id_type=MESH)
    n_peers = sum(present.astype(jnp.int32) for present, _ in peers)

    load_c = [pltpu.make_async_copy(c_hbm.at[e], c.at[e], sems.at[1 + e]) for e in range(3)]

    def message(to, m):
        if m == SMALL:
            return pltpu.make_async_remote_copy(
                src_ref=ssmall, dst_ref=rsmall.at[to], send_sem=small_send.at[to], recv_sem=small_recv.at[to],
                device_id=sends_to[to], device_id_type=MESH)
        return pltpu.make_async_remote_copy(
            src_ref=sbuf.at[m], dst_ref=rbuf.at[to, m], send_sem=send_sem.at[to, m], recv_sem=recv_sem.at[to, m],
            device_id=sends_to[to], device_id_type=MESH)

    def to_passer(m):
        return pltpu.make_async_remote_copy(
            src_ref=sbuf.at[m], dst_ref=pbuf.at[m - 1], send_sem=send_sem.at[CROSS, m], recv_sem=pass_recv.at[m - 1],
            device_id=at(passer), device_id_type=MESH)

    def passed_on(m):
        return pltpu.make_async_remote_copy(
            src_ref=pbuf.at[m - 1], dst_ref=rbuf.at[CROSS, m], send_sem=pass_send.at[m - 1],
            recv_sem=recv_sem.at[CROSS, m], device_id=at(receiver), device_id_type=MESH)

    def send(m):
        if m in (0, SMALL):
            @pl.when(has_cross)
            def _():
                message(CROSS, m).start()
        else:
            @pl.when(has_cross & (m < 4 - n_passed))
            def _():
                message(CROSS, m).start()

            @pl.when(m >= 4 - n_passed)
            def _():
                to_passer(m).start()
        for to in (BELOW, PARTNER):
            @pl.when(sends[to])
            def _():
                message(to, m).start()

    def pass_on(m):
        @pl.when(m >= 4 - n_passing)
        def _():
            to_passer(m).wait_recv()
            passed_on(m).start()

    load_n.wait()
    n = n_ref[0, 0, 0]
    strip = 16

    def strip_at(i):
        return pl.ds(pl.multiple_of(i * strip, strip), strip)

    def mask_rows(i, most):
        keep = jnp.where(tri((strip, 128))[0] + i * strip < n, 1.0, 0.0).astype(BF)
        kept = g[strip_at(i), :] * jnp.concatenate([keep] * (width // 128), axis=1)
        g[strip_at(i), :] = kept
        return jnp.maximum(most, jnp.abs(kept))

    most = jnp.zeros((strip, width), BF)
    for i, copy in enumerate(load_f):
        copy.wait()
        most = lax.fori_loop(i * rows // strip, (i + 1) * rows // strip, mask_rows, most, unroll=2)
    for copy in load_c:
        copy.start()
    most = jnp.max(most.astype(F32), axis=0, keepdims=True)
    power = jnp.clip(jnp.floor(jnp.log2(jnp.maximum(most, 1e-36))), -120.0, 120.0)
    scale, inverse = jnp.exp2(power).astype(BF).astype(F32), jnp.exp2(-power)
    column = jnp.where(tri((1, width))[1] < n, inverse, 0.0)
    column = jnp.broadcast_to(column, (strip, width)).astype(BF)

    @pl.loop(0, g.shape[0] // strip, unroll=4)
    def _(i):
        g[strip_at(i), :] = g[strip_at(i), :] * column

    sbuf[0] = gram(g, 0, 1, 3).astype(BF)
    pl.semaphore_wait(barrier, n_peers)
    send(0)
    sbuf[1, :, :B] = gram(g, 0, 3, 4).astype(BF)
    low0 = gram(g, 0, 0, 1)
    d0 = half_diagonal(low0)
    h1 = gram(g, 1, 1, 4)
    sbuf[1, :, B:] = packed(low0, h1[:, :B]).astype(BF)
    sbuf[3] = h1[:, B:].astype(BF)
    h2 = gram(g, 2, 2, 4)
    sbuf[2, :, :B] = h2[:, B:].astype(BF)
    low2 = h2[:, :B]
    d2 = half_diagonal(low2)
    lines = [scale[:, 128 * p:128 * (p + 1)] for p in range(8)]
    lines += [d0[:, :128], d0[:, 128:], d2[:, :128], d2[:, 128:]]
    for p, line in enumerate(lines):
        ssmall[p:p + 1, :] = line
    ssmall[12:16, :] = jnp.zeros((4, 128), F32)
    send(SMALL)
    send(1)
    sbuf[2, :, B:] = packed(low2, gram(g, 3, 3, 4)).astype(BF)
    send(2)
    send(3)

    def scale_c(frm):
        slot = slot_of[frm]
        for p in range(8):
            line = rsmall[frm, p:p + 1, :]
            column = jnp.transpose(jnp.broadcast_to(line, (128, 128))).astype(BF)
            at_rows = pl.ds(128 * p, 128)

            @pl.loop(0, 8, unroll=4)
            def _(q):
                cols = pl.ds(pl.multiple_of(q * 128, 128), 128)
                c[slot, at_rows, cols] = c[slot, at_rows, cols] * column

    def half_block(frm, u):
        row, col = tri((B, B))
        both = rbuf[frm, 1 if u < 2 else 2, :, B:].astype(F32)
        if u % 2 == 1:
            half[...] = jnp.where(row <= col, both, 0.0).astype(BF)
        else:
            line = jnp.concatenate([rsmall[frm, 8 + u:9 + u, :], rsmall[frm, 9 + u:10 + u, :]], axis=1)
            half[...] = jnp.where(row > col, both, jnp.where(row == col, jnp.broadcast_to(line, (B, B)), 0.0)).astype(BF)

    def beside(frm, u):
        return {
            0: [(rbuf.at[frm, 0], 1, 3), (rbuf.at[frm, 1, :, pl.ds(0, B)], 3, 4)],
            1: [(rbuf.at[frm, 3], 2, 4)],
            2: [(rbuf.at[frm, 2, :, pl.ds(0, B)], 3, 4)],
            3: [],
        }[u]

    def product(frm, u):
        slot = slot_of[frm]
        half_block(frm, u)
        for nt in range(2):
            cols = slice(512 * nt, 512 * (nt + 1))
            acc = jnp.dot(half[...], c[slot, u * B:(u + 1) * B, cols], preferred_element_type=F32)
            for factor, lo, hi in beside(frm, u):
                acc += jnp.dot(factor[...], c[slot, lo * B:hi * B, cols], preferred_element_type=F32)
            z[u * B:(u + 1) * B, cols] = acc.astype(BF)

    def product_t(u):
        half_block(CROSS, u)
        for i in range(4):
            rows_i = slice(i * B, (i + 1) * B)
            acc = lax.dot_general(ct[rows_i, u * B:(u + 1) * B], half[...], NT, preferred_element_type=F32)
            for factor, lo, hi in beside(CROSS, u):
                acc += lax.dot_general(ct[rows_i, lo * B:hi * B], factor[...], NT, preferred_element_type=F32)
            zt[rows_i, u * B:(u + 1) * B] = acc.astype(BF)

    def wait_for(frm, *messages):
        for m in messages:
            message(frm, m).wait_recv()

    def prepare(frm):
        wait_for(frm, 0, SMALL, 1)
        scale_c(frm)
        product(frm, 0)

    def add_up(frm, first):
        slot = slot_of[frm]

        @pl.loop(0, 4)
        def _(i):
            cols = pl.ds(pl.multiple_of(i * B, B), B)
            added = lax.dot_general(c[slot, :, cols], z[...], TN, preferred_element_type=F32)
            t_ref[cols, :] = added if first else t_ref[cols, :] + added

    for copy in load_c:
        copy.wait()
    prepare(PARTNER)
    wait_for(PARTNER, 2)
    product(PARTNER, 2)
    product(PARTNER, 3)
    pass_on(1)
    wait_for(PARTNER, 3)
    product(PARTNER, 1)
    pass_on(2)
    add_up(PARTNER, True)
    pass_on(3)

    @pl.when(has_cross)
    def _():
        wait_for(CROSS, 0, SMALL)
        scale_c(CROSS)
        slot = slot_of[CROSS]

        @pl.loop(0, 4)
        def _(k):
            block = pl.ds(pl.multiple_of(k * B, B), B)
            for i in range(4):
                ct[i * B:(i + 1) * B, block] = jnp.transpose(c[slot, block, i * B:(i + 1) * B])

    @pl.when(has_below)
    def _():
        prepare(BELOW)
        wait_for(BELOW, 2)
        product(BELOW, 2)
        product(BELOW, 3)
        wait_for(BELOW, 3)
        product(BELOW, 1)
        add_up(BELOW, False)

    @pl.when(has_cross)
    def _():
        wait_for(CROSS, 1)
        product_t(0)

        @pl.loop(0, 4)
        def _(i):
            cols = pl.ds(pl.multiple_of(i * B, B), B)
            t_ref[cols, :] += lax.dot_general(ct[cols, :B], zt[:, :B], NT, preferred_element_type=F32)

        half_block(CROSS, 1)
        for i in range(4):
            rows_i = slice(i * B, (i + 1) * B)
            zp[rows_i, :] = lax.dot_general(ct[rows_i, B:2 * B], half[...], NT, preferred_element_type=F32)

    for gap in range(4):
        @pl.loop(0, 4 - gap)
        def _(i):
            one = pl.ds(pl.multiple_of(i * B, B), B)
            two = pl.ds(pl.multiple_of((i + gap) * B, B), B)
            upper, lower = t_ref[one, two], t_ref[two, one]
            t_ref[one, two] = upper + jnp.transpose(lower)
            if gap:
                t_ref[two, one] = lower + jnp.transpose(upper)

    @pl.when(has_cross)
    def _():
        wait_for(CROSS, 2)
        product_t(2)
        product_t(3)

        @pl.loop(0, 4)
        def _(i):
            cols = pl.ds(pl.multiple_of(i * B, B), B)
            added = lax.dot_general(ct[cols, 2 * B:], zt[:, 2 * B:], NT, preferred_element_type=F32)
            added += lax.dot_general(zt[cols, 2 * B:], ct[:, 2 * B:], NT, preferred_element_type=F32)
            t_ref[cols, :] += added

    @pl.when(has_cross)
    def _():
        left[:, :B] = ct[:, B:2 * B]
        right[:, B:] = ct[:, B:2 * B]
        wait_for(CROSS, 3)
        for i in range(4):
            cols = slice(i * B, (i + 1) * B)
            acc = zp[cols, :] + lax.dot_general(ct[cols, 2 * B:], rbuf[CROSS, 3], NT, preferred_element_type=F32)
            acc = acc.astype(BF)
            left[cols, B:] = acc
            right[cols, :B] = acc

    @pl.when(jnp.logical_not(has_cross))
    def _():
        left[...] = jnp.zeros_like(left)
        right[...] = jnp.zeros_like(right)

    for to in (CROSS, PARTNER, BELOW):
        @pl.when(sends[to])
        def _():
            for m in range(5):
                message(to, m).wait_send()
    for m in (1, 2, 3):
        @pl.when(m >= 4 - n_passing)
        def _():
            passed_on(m).wait_send()


def last_part(t_ref, left, right, s_hbm, s, sems):
    tile = s.shape[1] // sems.shape[0]
    copies = []
    for i in range(sems.shape[0]):
        at = pl.ds(i * tile, tile)
        s[:, at] = t_ref[:, at] + lax.dot_general(left[...], right[at, :], NT, preferred_element_type=F32)
        copies.append(pltpu.make_async_copy(s.at[:, at], s_hbm.at[0, :, at], sems.at[i]))
        copies[-1].start()
    for copy in copies:
        copy.wait()


def on_device(factor_inv, sep_sizes, coupling):
    width, m = factor_inv.shape[1], coupling.shape[2]
    parts = pl.pallas_call(
        exchange,
        out_shape=(pltpu.VMEM((m, m), F32), pltpu.VMEM((m, 2 * B), BF), pltpu.VMEM((m, 2 * B), BF)),
        in_specs=[pl.BlockSpec(memory_space=pltpu.HBM)] * 3,
        out_specs=(pl.BlockSpec(memory_space=pltpu.VMEM),) * 3,
        scratch_shapes=[
            pltpu.VMEM((width, width), BF),
            pltpu.VMEM((3, width, m), BF),
            pltpu.VMEM((width, m), BF),
            pltpu.VMEM((B, B), BF),
            pltpu.VMEM((m, width), BF),
            pltpu.VMEM((m, width), BF),
            pltpu.VMEM((m, B), F32),
            pltpu.SMEM((1, 1, 1), jnp.int32),
            pltpu.VMEM((4, B, 2 * B), BF),
            pltpu.VMEM((16, 128), F32),
            pltpu.VMEM((3, 4, B, 2 * B), BF),
            pltpu.VMEM((3, 16, 128), F32),
            pltpu.VMEM((3, B, 2 * B), BF),
            pltpu.SemaphoreType.DMA((8,)),
            pltpu.SemaphoreType.DMA((4,)),
            pltpu.SemaphoreType.DMA((3, 4)),
            pltpu.SemaphoreType.DMA((3, 4)),
            pltpu.SemaphoreType.DMA((3,)),
            pltpu.SemaphoreType.DMA((3,)),
            pltpu.SemaphoreType.DMA((4,)),
            pltpu.SemaphoreType.DMA((4,)),
        ],
        compiler_params=pltpu.CompilerParams(collective_id=0, has_side_effects=True, vmem_limit_bytes=54 * 1024 * 1024),
        name="exchange",
    )(factor_inv, sep_sizes, coupling)
    return pl.pallas_call(
        last_part,
        out_shape=jax.ShapeDtypeStruct((1, m, m), F32),
        in_specs=[pl.BlockSpec(memory_space=pltpu.VMEM)] * 3,
        out_specs=pl.BlockSpec(memory_space=pl.ANY),
        scratch_shapes=[pltpu.VMEM((m, m), F32), pltpu.SemaphoreType.DMA((4,))],
        compiler_params=pltpu.CompilerParams(vmem_limit_bytes=8 * 1024 * 1024),
        name="last_part",
    )(*parts)


def solution(mesh):
    spec = P("gx", "gy", "gz")
    return jax.shard_map(on_device, mesh=mesh, in_specs=(spec, spec, spec), out_specs=spec, check_vma=False)
```

time: 57.1 us -> 54.4 us (0.953)
  local copies, waits for them, and re-layouts: 2.02 us -> 0 us
    unnamed x1 -> x0, local copies, waits for them, and re-layouts: 2.02 us -> none
    pallas_call x1 -> x2, Pallas kernels: 54.1 us -> 53.6 us  [the longest x1 50.8 us: on_device(): pl.pallas_call(exchange, out_shape=(pltpu.VMEM((m, m), F32), pltpu.VMEM((...]
where the time goes in v2:
time: 54.4 us; the launch traced here: 54.3 us
  Pallas kernels  53.6 us (99%)
  between operations  0.66 us (1%)
    pallas_call x1, Pallas kernels, on_device(): pl.pallas_call(exchange, out_shape=(pltpu.VMEM((m, m), F32), pltpu.VMEM((...  50.8 us
    pallas_call x1, Pallas kernels, on_device(): pl.pallas_call(last_part, out_shape=jax.ShapeDtypeStruct((1, m, m), F32),...  2.84 us

profile of v2, /device:TPU:45, one launch (start us, length us, event | category | flops | bytes accessed | tf_op | source)
XLA Modules:
  0.0 54.3 jit_solution(10444957516095282225)
XLA Ops:
  0.7 50.8 %exchange.1 = (f32[1024,1024]{1,0:T(8,128)S(1)}, bf16[1024,512]{1,0:T(8,128)(2,1)S(1)}, bf16[1024,512]{1,0:T(8,128)(2,1)S(1)}) custom-call(bf16[1,1024,1024]{2,1,0:T(8,128)(2,1)} %f_hbm.1, s32[1,1,1]{2,1,0:T(1,128)S(6)} %copy.4.n_hbm, bf16[3,1024,1024]{2,1,0:T(8,128)(2,1)} %c_hbm.1), custom_call_target="tpu_custom_call" | custom-call | tf_op jit(solution)/shard_map/exchange/pallas_call | solution.py:360
  51.4 2.8 %last_part.1 = f32[1,1024,1024]{2,1,0:T(8,128)} custom-call(f32[1024,1024]{1,0:T(8,128)S(1)} %get-tuple-element.8.t_ref, bf16[1024,512]{1,0:T(8,128)(2,1)S(1)} %get-tuple-element.9.left, bf16[1024,512]{1,0:T(8,128)(2,1)S(1)} %get-tuple-element.10.right), custom_call_target="tpu_custom_call" | custom-call | tf_op jit(solution)/shard_map/last_part/pallas_call | solution.py:391

commit v3 on v2

--- a/solution.py
+++ b/solution.py
@@ -148,13 +148,16 @@
     column = jnp.where(tri((1, width))[1] < n, inverse, 0.0)
     column = jnp.broadcast_to(column, (strip, width)).astype(BF)
 
-    @pl.loop(0, g.shape[0] // strip, unroll=4)
-    def _(i):
-        g[strip_at(i), :] = g[strip_at(i), :] * column
-
+    def scale_g(cols):
+        @pl.loop(0, g.shape[0] // strip, unroll=4)
+        def _(i):
+            g[strip_at(i), cols] = g[strip_at(i), cols] * column[:, cols]
+
+    scale_g(slice(0, 3 * B))
     sbuf[0] = gram(g, 0, 1, 3).astype(BF)
     pl.semaphore_wait(barrier, n_peers)
     send(0)
+    scale_g(slice(3 * B, width))
     sbuf[1, :, :B] = gram(g, 0, 3, 4).astype(BF)
     low0 = gram(g, 0, 0, 1)
     d0 = half_diagonal(low0)
@@ -167,9 +170,7 @@
     d2 = half_diagonal(low2)
     lines = [scale[:, 128 * p:128 * (p + 1)] for p in range(8)]
     lines += [d0[:, :128], d0[:, 128:], d2[:, :128], d2[:, 128:]]
-    for p, line in enumerate(lines):
-        ssmall[p:p + 1, :] = line
-    ssmall[12:16, :] = jnp.zeros((4, 128), F32)
+    ssmall[...] = jnp.concatenate(lines + [jnp.zeros((4, 128), F32)], axis=0).astype(BF)
     send(SMALL)
     send(1)
     sbuf[2, :, B:] = packed(low2, gram(g, 3, 3, 4)).astype(BF)
@@ -178,8 +179,9 @@
 
     def scale_c(frm):
         slot = slot_of[frm]
+        lines = rsmall[frm].astype(F32)
         for p in range(8):
-            line = rsmall[frm, p:p + 1, :]
+            line = lines[p:p + 1, :]
             column = jnp.transpose(jnp.broadcast_to(line, (128, 128))).astype(BF)
             at_rows = pl.ds(128 * p, 128)
 
@@ -194,7 +196,8 @@
         if u % 2 == 1:
             half[...] = jnp.where(row <= col, both, 0.0).astype(BF)
         else:
-            line = jnp.concatenate([rsmall[frm, 8 + u:9 + u, :], rsmall[frm, 9 + u:10 + u, :]], axis=1)
+            lines = rsmall[frm].astype(F32)
+            line = jnp.concatenate([lines[8 + u:9 + u, :], lines[9 + u:10 + u, :]], axis=1)
             half[...] = jnp.where(row > col, both, jnp.where(row == col, jnp.broadcast_to(line, (B, B)), 0.0)).astype(BF)
 
     def beside(frm, u):
@@ -344,12 +347,12 @@
 
 
 def last_part(t_ref, left, right, s_hbm, s, sems):
-    tile = s.shape[1] // sems.shape[0]
+    tile = s.shape[0] // sems.shape[0]
     copies = []
     for i in range(sems.shape[0]):
         at = pl.ds(i * tile, tile)
-        s[:, at] = t_ref[:, at] + lax.dot_general(left[...], right[at, :], NT, preferred_element_type=F32)
-        copies.append(pltpu.make_async_copy(s.at[:, at], s_hbm.at[0, :, at], sems.at[i]))
+        s[at, :] = t_ref[at, :] + lax.dot_general(left[at, :], right[...], NT, preferred_element_type=F32)
+        copies.append(pltpu.make_async_copy(s.at[at], s_hbm.at[0, at], sems.at[i]))
         copies[-1].start()
     for copy in copies:
         copy.wait()
@@ -372,9 +375,9 @@
             pltpu.VMEM((m, B), F32),
             pltpu.SMEM((1, 1, 1), jnp.int32),
             pltpu.VMEM((4, B, 2 * B), BF),
-            pltpu.VMEM((16, 128), F32),
+            pltpu.VMEM((16, 128), BF),
             pltpu.VMEM((3, 4, B, 2 * B), BF),
-            pltpu.VMEM((3, 16, 128), F32),
+            pltpu.VMEM((3, 16, 128), BF),
             pltpu.VMEM((3, B, 2 * B), BF),
             pltpu.SemaphoreType.DMA((8,)),
             pltpu.SemaphoreType.DMA((4,)),

time: 54.4 us -> 53.9 us (level)
  no operation moved by 1% of the time
where the time goes in v3:
time: 53.9 us; the launch traced here: 53.8 us
  Pallas kernels  53.1 us (99%)
  between operations  0.66 us (1%)
    pallas_call x1, Pallas kernels, on_device(): pl.pallas_call(exchange, out_shape=(pltpu.VMEM((m, m), F32), pltpu.VMEM((...  50.6 us
    pallas_call x1, Pallas kernels, on_device(): pl.pallas_call(last_part, out_shape=jax.ShapeDtypeStruct((1, m, m), F32),...  2.51 us

profile of v3, /device:TPU:45, one launch (start us, length us, event | category | flops | bytes accessed | tf_op | source)
XLA Modules:
  0.0 53.8 jit_solution(10430805607592399861)
XLA Ops:
  0.7 50.6 %exchange.1 = (f32[1024,1024]{1,0:T(8,128)S(1)}, bf16[1024,512]{1,0:T(8,128)(2,1)S(1)}, bf16[1024,512]{1,0:T(8,128)(2,1)S(1)}) custom-call(bf16[1,1024,1024]{2,1,0:T(8,128)(2,1)} %f_hbm.1, s32[1,1,1]{2,1,0:T(1,128)S(6)} %copy.4.n_hbm, bf16[3,1024,1024]{2,1,0:T(8,128)(2,1)} %c_hbm.1), custom_call_target="tpu_custom_call" | custom-call | tf_op jit(solution)/shard_map/exchange/pallas_call | solution.py:363
  51.2 2.5 %last_part.1 = f32[1,1024,1024]{2,1,0:T(8,128)} custom-call(f32[1024,1024]{1,0:T(8,128)S(1)} %get-tuple-element.8.t_ref, bf16[1024,512]{1,0:T(8,128)(2,1)S(1)} %get-tuple-element.9.left, bf16[1024,512]{1,0:T(8,128)(2,1)S(1)} %get-tuple-element.10.right), custom_call_target="tpu_custom_call" | custom-call | tf_op jit(solution)/shard_map/last_part/pallas_call | solution.py:394

commit v4 on v3

--- a/solution.py
+++ b/solution.py
@@ -139,7 +139,7 @@
     most = jnp.zeros((strip, width), BF)
     for i, copy in enumerate(load_f):
         copy.wait()
-        most = lax.fori_loop(i * rows // strip, (i + 1) * rows // strip, mask_rows, most, unroll=2)
+        most = lax.fori_loop(i * rows // strip, (i + 1) * rows // strip, mask_rows, most, unroll=8)
     for copy in load_c:
         copy.start()
     most = jnp.max(most.astype(F32), axis=0, keepdims=True)
@@ -149,7 +149,7 @@
     column = jnp.broadcast_to(column, (strip, width)).astype(BF)
 
     def scale_g(cols):
-        @pl.loop(0, g.shape[0] // strip, unroll=4)
+        @pl.loop(0, g.shape[0] // strip, unroll=16)
         def _(i):
             g[strip_at(i), cols] = g[strip_at(i), cols] * column[:, cols]
 

time: 53.9 us -> 53.9 us (level)
  no operation moved by 1% of the time
where the time goes in v4:
time: 53.9 us; the launch traced here: 53.8 us
  Pallas kernels  53.1 us (99%)
  between operations  0.66 us (1%)
    pallas_call x1, Pallas kernels, on_device(): pl.pallas_call(exchange, out_shape=(pltpu.VMEM((m, m), F32), pltpu.VMEM((...  50.6 us
    pallas_call x1, Pallas kernels, on_device(): pl.pallas_call(last_part, out_shape=jax.ShapeDtypeStruct((1, m, m), F32),...  2.51 us

profile of v4, /device:TPU:45, one launch (start us, length us, event | category | flops | bytes accessed | tf_op | source)
XLA Modules:
  0.0 53.8 jit_solution(12016810217393903853)
XLA Ops:
  0.7 50.6 %exchange.1 = (f32[1024,1024]{1,0:T(8,128)S(1)}, bf16[1024,512]{1,0:T(8,128)(2,1)S(1)}, bf16[1024,512]{1,0:T(8,128)(2,1)S(1)}) custom-call(bf16[1,1024,1024]{2,1,0:T(8,128)(2,1)} %f_hbm.1, s32[1,1,1]{2,1,0:T(1,128)S(6)} %copy.4.n_hbm, bf16[3,1024,1024]{2,1,0:T(8,128)(2,1)} %c_hbm.1), custom_call_target="tpu_custom_call" | custom-call | tf_op jit(solution)/shard_map/exchange/pallas_call | solution.py:363
  51.3 2.5 %last_part.1 = f32[1,1024,1024]{2,1,0:T(8,128)} custom-call(f32[1024,1024]{1,0:T(8,128)S(1)} %get-tuple-element.8.t_ref, bf16[1024,512]{1,0:T(8,128)(2,1)S(1)} %get-tuple-element.9.left, bf16[1024,512]{1,0:T(8,128)(2,1)S(1)} %get-tuple-element.10.right), custom_call_target="tpu_custom_call" | custom-call | tf_op jit(solution)/shard_map/last_part/pallas_call | solution.py:394
